TPU v7x, 256 devices: a whole 4x4x8 slice. The times are simulated.
256 devices in a mesh: tok: 8 (over x, core), col: 32 (over y, z).
Axes of the slice: x: 4, y: 4, z: 8, core: 2. Of those that a mesh axis runs over, the one named last changes fastest.
Arguments:
- hidden_in: bfloat16 [2048, 36864], P('tok', 'col'), may hold values from -6 to 6
- down_weight: bfloat16 [4608, 36864], P('col', 'tok'), may hold values from -0.046875 to 0.046875
- keep_mask: int32 [4608, 36864], P('col', 'tok'), may hold values 0 or 1
Outputs:
- layer_out: bfloat16 [2048, 4608], P(('tok', 'col'))
- hessian: float32 [4608, 4608], P('col', 'tok')
All inputs are finite; a program needn't handle non-finite values. No bound on the sum of `keep_mask` on one device may be relied on, other than what follows from the above.
Results may differ from a plain program's by a relative error of at most 0.012.
Values may be sent and summed in bfloat16 or wider, within the bound.
A program may use at most 128 MiB of HBM per device.

v0:
```python
import jax
import jax.numpy as jnp
from jax import lax
from jax.sharding import PartitionSpec as P


def laid_out(pieces, dim):
    lengths = list(pieces.shape[1:])
    lengths[dim] *= pieces.shape[0]
    return jnp.moveaxis(pieces, 0, dim).reshape(lengths)


def from_everyone(x, axis):
    size = lax.axis_size(axis)
    return lax.all_to_all(jnp.broadcast_to(x[None], (size, *x.shape)), axis, 0, 0, tiled=True)


def gathered_copies(x, axis, dim):
    return laid_out(from_everyone(x, axis), dim)


def split_up(x, dim, size):
    before, after = (x.shape[:dim], x.shape[dim + 1 :])
    return jnp.moveaxis(x.reshape(*before, size, -1, *after), dim, 0)


def sent_and_summed(x, axis, dim):
    pieces = split_up(x, dim, lax.axis_size(axis))
    arrived = lax.all_to_all(pieces, axis, split_axis=0, concat_axis=0, tiled=True)
    return arrived.astype(jnp.float32).sum(axis=0)


def contract_rows(left, right):
    return lax.dot_general(
        left, right, (((0,), (0,)), ((), ())), preferred_element_type=jnp.float32
    )


def contract_last(left, right):
    return lax.dot_general(
        left, right, (((1,), (1,)), ((), ())), preferred_element_type=jnp.float32
    )


def body(hidden_in, down_weight, keep_mask):
    pruned = down_weight * keep_mask.astype(down_weight.dtype)
    all_features = lax.all_gather(hidden_in, "col", axis=1, tiled=True)
    summed = contract_last(all_features, lax.all_gather(pruned, "tok", axis=1, tiled=True))
    layer_cols = summed.astype(jnp.bfloat16)
    scaling = 2.0 / (layer_cols.shape[0] * lax.axis_size("tok"))
    whole = gathered_copies(layer_cols, "col", 1)
    share_rows = whole.shape[0] // lax.axis_size("col")
    layer_out = lax.dynamic_slice_in_dim(whole, lax.axis_index("col") * share_rows, share_rows, 0)
    hessian_term = contract_rows(layer_cols, whole)
    hessian = sent_and_summed((hessian_term * scaling).astype(jnp.bfloat16), "tok", 1)
    return (layer_out, hessian)


def solution(mesh):
    in_specs = (P("tok", "col"), P("col", "tok"), P("col", "tok"))
    out_specs = (P(("tok", "col"), None), P("col", "tok"))
    return jax.shard_map(body, mesh=mesh, in_specs=in_specs, out_specs=out_specs, check_vma=False)
```

profile of v0, /device:TPU:1, one launch (start us, length us, event | category | flops | bytes accessed | tf_op | source)
XLA Modules:
  0.0 347.3 jit_solution(11855072798509974966)
XLA Ops:
  7.2 0.0 all-gather.3.cloned.1.call-start
  7.2 3.4 convert_multiply_fusion
  10.7 0.0 all-gather.3.cloned.1.call-update
  10.7 0.0 all-gather.5.cloned.1.call-start
  10.7 0.7 all-gather.5.cloned.1.call-update
  11.4 65.1 %all-gather.3.cloned.1.call-done = bf16[144,36864]{1,0:T(8,128)(2,1)} async-done(((bf16[144,4608]{1,0:T(8,128)(2,1)}), bf16[144,36864]{1,0:T(8,128)(2,1)}) %all-gather.3.cloned.1.call-update) | async-done | bytes 10616848 | tf_op jit(solution)/shard_map/all_gather | solution.py:48
  76.6 152.6 %all-gather.5.cloned.1.call-done = bf16[256,36864]{1,0:T(8,128)(2,1)} async-done(((bf16[256,1152]{1,0:T(8,128)(2,1)}), bf16[256,36864]{1,0:T(8,128)(2,1)}) %all-gather.5.cloned.1.call-update) | async-done | bytes 18874384 | tf_op jit(solution)/shard_map/all_gather | solution.py:47
  229.1 12.8 %convolution_convert_fusion = bf16[144,256]{1,0:T(8,128)(2,1)S(1)} fusion(bf16[144,36864]{1,0:T(8,128)(2,1)} %all-gather.3.cloned.1.call-done, bf16[256,36864]{1,0:T(8,128)(2,1)} %all-gather.5.cloned.1.call-done), kind=kOutput, calls=%fused_computation.5 | convolution fusion | flops 2717945856 | bytes 29564928 | tf_op jit(solution)/shard_map/dot_general | solution.py:40
  241.9 0.2 broadcast_in_dim.2
  242.1 58.9 %all_to_all.10 = bf16[32,256,144]{1,2,0:T(8,128)(2,1)S(1)} all-to-all(bf16[32,256,144]{1,2,0:T(8,128)(2,1)S(1)} %broadcast_in_dim.2), channel_id=1, replica_groups=mesh['tok'=8,'col'=32] {'col'}, dimensions={0} | all-to-all | bytes 4718592 | tf_op jit(solution)/shard_map/all_to_all | solution.py:15
  300.9 2.0 fusion
  303.0 3.7 %reshape.12 = bf16[144,8,576]{2,1,0:T(8,128)(2,1)} reshape(bf16[144,4608]{1,0:T(8,128)(2,1)} %fusion) | data formatting | bytes 2654208 | tf_op jit(solution)/shard_map/reshape | solution.py:24
  306.7 2.7 copy.10
  309.4 9.1 %all-to-all-start.1 = ((bf16[8,144,576]{2,1,0:T(8,128)(2,1)}), bf16[8,144,576]{2,1,0:T(8,128)(2,1)}, u32[]{:S(2)}, u32[]{:S(2)}) async-start(bf16[8,144,576]{2,1,0:T(8,128)(2,1)} %bitcast.13), calls=%async_computation.1 | async-start | bytes 2949120 | tf_op jit(solution)/shard_map/all_to_all | solution.py:29
  318.4 0.4 constant_dynamic-slice_fusion
  318.8 1.0 copy.8
  319.8 18.3 %all-to-all-done.1 = bf16[8,144,576]{2,1,0:T(8,128)(2,1)} async-done(((bf16[8,144,576]{2,1,0:T(8,128)(2,1)}), bf16[8,144,576]{2,1,0:T(8,128)(2,1)}, u32[]{:S(2)}, u32[]{:S(2)}) %all-to-all-start.1) | async-done | bytes 1327136 | tf_op jit(solution)/shard_map/all_to_all | solution.py:29
  338.1 2.4 convert_reduce_fusion
Async XLA Ops:
  7.2 69.4 %all-gather.3.cloned.1.call-start = ((), (), s32[]{:S(2)}) async-start(), calls=%async_computation.2 | async-start | bytes 11943936 | tf_op jit(solution)/shard_map/all_gather | solution.py:48
  10.7 218.5 %all-gather.5.cloned.1.call-start = ((), (), s32[]{:S(2)}) async-start(), calls=%async_computation.3 | async-start | bytes 19464192 | tf_op jit(solution)/shard_map/all_gather | solution.py:47
  309.4 28.7 %all-to-all-start.1 = ((bf16[8,144,576]{2,1,0:T(8,128)(2,1)}), bf16[8,144,576]{2,1,0:T(8,128)(2,1)}, u32[]{:S(2)}, u32[]{:S(2)}) async-start(bf16[8,144,576]{2,1,0:T(8,128)(2,1)} %bitcast.13), calls=%async_computation.1 | async-start | bytes 2949120 | tf_op jit(solution)/shard_map/all_to_all | solution.py:29
Sparse Core Ops, SparseCore 0:
  10.8 65.7 all-gather.2
  79.3 149.8 all-gather.4
where the time goes:
time: 348 us; the launch traced here: 347 us
  waiting for transfers between devices  237 us (68%)
  blocking collectives  58.9 us (17%)
  matrix products  14.8 us (4%)
  between operations  14.1 us (4%)
  starting transfers between devices  9.16 us (3%)
  local copies, waits for them, and re-layouts  7.93 us (2%)
  other arithmetic  5.8 us (2%)
    all_gather x1, waiting for transfers between devices, body(): all_features = lax.all_gather(hidden_in, 'col', axis=1, tiled=True)  153 us
    all_gather x1, waiting for transfers between devices, body(): lax.all_gather(pruned, 'tok', axis=1, tiled=True)  65.1 us
    all_to_all x1, blocking collectives, from_everyone(): lax.all_to_all(jnp.broadcast_to(x[None], (size, *x.shape)), axis, 0, 0, t...  58.9 us
    all_to_all x1, waiting for transfers between devices, sent_and_summed(): lax.all_to_all(pieces, axis, split_axis=0, concat_axis=0, tiled=True)  18.3 us
    dot_general x1, matrix products, contract_last(): lax.dot_general(left, right, (((1,), (1,)), ((), ())), preferred_element_...  12.8 us
    all_to_all x1, starting transfers between devices, sent_and_summed(): lax.all_to_all(pieces, axis, split_axis=0, concat_axis=0, tiled=True)  9.08 us
  transfers between devices with their start and end apart: 3, of which 3 were waited for; matrix products, arithmetic and copies ran while one was open for 0% of the time, Pallas kernels for 0%

commit v1 on v0

--- a/solution.py
+++ b/solution.py
@@ -2,6 +2,12 @@
 import jax.numpy as jnp
 from jax import lax
 from jax.sharding import PartitionSpec as P
+
+
+def tiled_gather(x, axis, dim):
+    length = lax.axis_size(axis)
+    repeats = [length if d == dim else 1 for d in range(x.ndim)]
+    return lax.all_to_all(jnp.tile(x, repeats), axis, split_axis=dim, concat_axis=dim, tiled=True)
 
 
 def laid_out(pieces, dim):
@@ -45,7 +51,7 @@
 def body(hidden_in, down_weight, keep_mask):
     pruned = down_weight * keep_mask.astype(down_weight.dtype)
     all_features = lax.all_gather(hidden_in, "col", axis=1, tiled=True)
-    summed = contract_last(all_features, lax.all_gather(pruned, "tok", axis=1, tiled=True))
+    summed = contract_last(all_features, tiled_gather(pruned, "tok", 1))
     layer_cols = summed.astype(jnp.bfloat16)
     scaling = 2.0 / (layer_cols.shape[0] * lax.axis_size("tok"))
     whole = gathered_copies(layer_cols, "col", 1)

time: 348 us -> 283 us (0.81)
  waiting for transfers between devices: 237 us -> 38.7 us
  blocking collectives: 58.9 us -> 184 us
  local copies, waits for them, and re-layouts: 7.93 us -> 17.5 us
    all_gather x1, waiting for transfers between devices: 153 us -> 19.8 us  [body(): all_features = lax.all_gather(hidden_in, 'col', axis=1, tiled=True)]
    all_to_all x0 -> x1, blocking collectives: none -> 125 us  [tiled_gather(): lax.all_to_all(jnp.tile(x, repeats), axis, split_axis=dim, concat_axis=di...]
    all_gather x1 -> x0, waiting for transfers between devices: 65.1 us -> none  [body(): lax.all_gather(pruned, 'tok', axis=1, tiled=True)]
    another operation x0 -> x1, local copies, waits for them, and re-layouts: none -> 4.87 us  [tiled_gather(): jnp.tile(x, repeats)]
    all_to_all x0 -> x1, local copies, waits for them, and re-layouts: none -> 4.73 us  [tiled_gather(): lax.all_to_all(jnp.tile(x, repeats), axis, split_axis=dim, concat_axis=di...]
  transfers between devices with their start and end apart: 3 -> 2, of which waited for: 3 -> 2; matrix products, arithmetic and copies ran while one was open for 0% -> 5% of each run, Pallas kernels for 0% -> 0%
where the time goes in v1:
time: 283 us
  blocking collectives  184 us (65%)
  waiting for transfers between devices  38.7 us (14%)
  local copies, waits for them, and re-layouts  17.5 us (6%)
  matrix products  14.8 us (5%)
  between operations  14.1 us (5%)
  starting transfers between devices  9.12 us (3%)
  other arithmetic  4.69 us (2%)
    all_to_all x1, blocking collectives, tiled_gather(): lax.all_to_all(jnp.tile(x, repeats), axis, split_axis=dim, concat_axis=di...  125 us
    all_to_all x1, blocking collectives, from_everyone(): lax.all_to_all(jnp.broadcast_to(x[None], (size, *x.shape)), axis, 0, 0, t...  58.9 us
    all_gather x1, waiting for transfers between devices, body(): all_features = lax.all_gather(hidden_in, 'col', axis=1, tiled=True)  19.8 us
    all_to_all x1, waiting for transfers between devices, sent_and_summed(): lax.all_to_all(pieces, axis, split_axis=0, concat_axis=0, tiled=True)  18.3 us
    dot_general x1, matrix products, contract_last(): lax.dot_general(left, right, (((1,), (1,)), ((), ())), preferred_element_...  12.8 us
    all_to_all x1, starting transfers between devices, sent_and_summed(): lax.all_to_all(pieces, axis, split_axis=0, concat_axis=0, tiled=True)  9.08 us
    reshape x2, local copies, waits for them, and re-layouts, split_up(): return jnp.moveaxis(x.reshape(*before, size, -1, *after), dim, 0)  6.41 us
  transfers between devices with their start and end apart: 2, of which 2 were waited for; matrix products, arithmetic and copies ran while one was open for 5% of the time, Pallas kernels for 0%

profile of v1, /device:TPU:1, one launch (start us, length us, event | category | flops | bytes accessed | tf_op | source)
XLA Modules:
  0.0 282.5 jit_solution(15644688889364216236)
XLA Ops:
  7.2 0.0 all-gather.2.cloned.1.call-start
  7.2 0.7 all-gather.2.cloned.1.call-update
  7.9 2.3 convert_multiply_fusion
  10.2 4.9 %tile.2 = bf16[144,8,4608]{2,0,1:T(8,128)(2,1)} broadcast(bf16[144,4608]{1,0:T(8,128)(2,1)S(1)} %convert_multiply_fusion), dimensions={0,2} | broadcast | bytes 11943936 | tf_op jit(solution)/shard_map/tile | solution.py:10
  15.1 124.8 %all_to_all.19 = bf16[144,8,4608]{2,0,1:T(8,128)(2,1)S(1)} all-to-all(bf16[144,8,4608]{2,0,1:T(8,128)(2,1)} %tile.2), channel_id=1, replica_groups=mesh['tok'=8,'col'=32] {'tok'}, dimensions={1} | all-to-all | bytes 21233664 | tf_op jit(solution)/shard_map/all_to_all | solution.py:10
  139.9 4.7 %copy.12 = bf16[8,18,8,4608]{3,2,0,1:T(8,128)(2,1)} copy(bf16[8,18,8,4608]{3,2,1,0:T(8,128)(2,1)S(1)} %bitcast.14) | data formatting | bytes 21233664 | tf_op jit(solution)/shard_map/all_to_all | solution.py:10
  144.6 19.8 %all-gather.2.cloned.1.call-done = bf16[256,36864]{1,0:T(8,128)(2,1)} async-done(((bf16[256,1152]{1,0:T(8,128)(2,1)}), bf16[256,36864]{1,0:T(8,128)(2,1)}) %all-gather.2.cloned.1.call-update) | async-done | bytes 18874384 | tf_op jit(solution)/shard_map/all_gather | solution.py:53
  164.4 12.8 %convolution_convert_fusion = bf16[144,256]{1,0:T(8,128)(2,1)S(1)} fusion(bf16[144,36864]{1,0:T(8,128)(2,1)} %bitcast.13, bf16[256,36864]{1,0:T(8,128)(2,1)} %all-gather.2.cloned.1.call-done), kind=kOutput, calls=%fused_computation.5 | convolution fusion | flops 2717945856 | bytes 29564928 | tf_op jit(solution)/shard_map/dot_general | solution.py:46
  177.2 0.2 broadcast_in_dim.2
  177.3 58.9 %all_to_all.20 = bf16[32,256,144]{1,2,0:T(8,128)(2,1)S(1)} all-to-all(bf16[32,256,144]{1,2,0:T(8,128)(2,1)S(1)} %broadcast_in_dim.2), channel_id=1, replica_groups=mesh['tok'=8,'col'=32] {'col'}, dimensions={0} | all-to-all | bytes 4718592 | tf_op jit(solution)/shard_map/all_to_all | solution.py:21
  236.2 2.0 fusion
  238.2 3.8 %reshape.19 = bf16[144,8,576]{2,1,0:T(8,128)(2,1)} reshape(bf16[144,4608]{1,0:T(8,128)(2,1)} %fusion) | data formatting | bytes 2654208 | tf_op jit(solution)/shard_map/reshape | solution.py:30
  242.0 2.7 copy.14
  244.6 9.1 %all-to-all-start.2 = ((bf16[8,144,576]{2,1,0:T(8,128)(2,1)}), bf16[8,144,576]{2,1,0:T(8,128)(2,1)}, u32[]{:S(2)}, u32[]{:S(2)}) async-start(bf16[8,144,576]{2,1,0:T(8,128)(2,1)} %bitcast.17), calls=%async_computation.2 | async-start | bytes 2949120 | tf_op jit(solution)/shard_map/all_to_all | solution.py:35
  253.7 0.4 constant_dynamic-slice_fusion
  254.1 1.0 copy.11
  255.1 18.3 %all-to-all-done.2 = bf16[8,144,576]{2,1,0:T(8,128)(2,1)} async-done(((bf16[8,144,576]{2,1,0:T(8,128)(2,1)}), bf16[8,144,576]{2,1,0:T(8,128)(2,1)}, u32[]{:S(2)}, u32[]{:S(2)}) %all-to-all-start.2) | async-done | bytes 1327136 | tf_op jit(solution)/shard_map/all_to_all | solution.py:35
  273.3 2.4 convert_reduce_fusion
Async XLA Ops:
  7.2 157.2 %all-gather.2.cloned.1.call-start = ((), (), s32[]{:S(2)}) async-start(), calls=%async_computation.3 | async-start | bytes 19464192 | tf_op jit(solution)/shard_map/all_gather | solution.py:53
  244.6 28.7 %all-to-all-start.2 = ((bf16[8,144,576]{2,1,0:T(8,128)(2,1)}), bf16[8,144,576]{2,1,0:T(8,128)(2,1)}, u32[]{:S(2)}, u32[]{:S(2)}) async-start(bf16[8,144,576]{2,1,0:T(8,128)(2,1)} %bitcast.17), calls=%async_computation.2 | async-start | bytes 2949120 | tf_op jit(solution)/shard_map/all_to_all | solution.py:35
Sparse Core Ops, SparseCore 0:
  10.7 153.6 all-gather.1
